TPU v7x, 32 devices: a whole 2x2x4 slice. The times are simulated.
32 devices in a mesh: rows: 8 (over y, x, core), feat: 4 (over z).
Axes of the slice: x: 2, y: 2, z: 4, core: 2. Of those that a mesh axis runs over, the one named last changes fastest.
Arguments:
- bins: int32 [8192, 512], P('rows', 'feat'), may hold values from -2147483648 to 2147483647, as said below
- hessian: float32 [32768], P('rows'), may hold values from 0.05 to 1
- thresholds: float32 [128], replicated, may hold values from 0.02 to 0.98
Outputs:
- cuts: float32 [512, 128], P('feat')
Inputs may be any that keep to these rules, and one draw needn't show every extreme that they name: `bins`: each word holds the bin ids, 0 to 255, of rows 4i to 4i + 3 of one feature, row 4i + k in bits 8k to 8k + 7 of the two's complement word.
All inputs are finite; a program needn't handle non-finite values.
Results may differ from a plain program's by a relative error of at most 0.000065.
Values sent between devices are 32-bit elements; how exact they have to be, the bound alone decides.
A program may use at most 192 MiB of HBM per device.

v0:
```python
import math
import jax
import jax.numpy as jnp
from jax import lax
from jax.sharding import PartitionSpec as P

BINS = 256


def unpack(words):
    parts = [jnp.bitwise_and(jnp.right_shift(words, 8 * k), 255) for k in range(4)]
    stacked = jnp.stack(parts, axis=1)
    return stacked.reshape(words.shape[0] * 4, words.shape[1])


def histogram(columns, weights):
    count, width = columns.shape
    limit = max(8, 1048576 // (width * 16))
    block = math.gcd(count, limit)
    col_blocks = columns.reshape(count // block, block, width)
    wt_blocks = weights.reshape(count // block, block)
    levels = jnp.arange(16, dtype=jnp.int32)

    def add_block(total, item):
        col_part, wt_part = item
        high = jnp.right_shift(col_part, 4)
        low = jnp.bitwise_and(col_part, 15)
        high_hot = jnp.where(high[:, :, None] == levels, wt_part[:, None, None], 0.0)
        low_hot = (low[:, :, None] == levels).astype(jnp.float32)
        joint = jnp.einsum("rkh,rkl->khl", high_hot, low_hot, precision=lax.Precision.HIGHEST)
        return (total + joint, None)

    start = jnp.zeros((width, 16, 16), jnp.float32)
    total, unused = lax.scan(add_block, start, (col_blocks, wt_blocks))
    return total.reshape(width, BINS)


def cut_positions(hist, thresholds):
    cum = jnp.cumsum(hist, axis=1)
    before = cum - hist
    total = cum[:, -1]
    target = thresholds[None, :, None] * total[:, None, None]
    ratio = (target - before[:, None, :]) / (hist[:, None, :] + 1.0)
    return jnp.sum(jnp.clip(ratio, 0.0, 1.0), axis=2)


def local(bins, hessian, thresholds):
    regrouped = lax.all_to_all(bins, "rows", split_axis=1, concat_axis=0, tiled=True)
    weights = lax.all_gather(hessian, "rows", axis=0, tiled=True)
    hist = histogram(unpack(regrouped), weights)
    cuts = cut_positions(hist, thresholds)
    return lax.all_gather(cuts, "rows", axis=0, tiled=True)


def solution(mesh):
    in_specs = (P("rows", "feat"), P("rows"), P())
    out_specs = P("feat", None)
    return jax.shard_map(local, mesh=mesh, in_specs=in_specs, out_specs=out_specs, check_vma=False)
```

profile of v0, /device:TPU:0, one launch (start us, length us, event | category | flops | bytes accessed | tf_op | source)
XLA Modules:
  0.0 84.6 jit_solution(17974510913110473244)
XLA Ops:
  0.0 0.0 copy-start
  0.0 2.0 %copy.34 = s32[1024,128]{0,1:T(8,128)} copy(s32[1024,128]{1,0:T(8,128)} %param.5) | data formatting | bytes 1048576 | tf_op args[0]
  2.0 5.2 %all-to-all-start = ((s32[1024,8,16]{0,2,1:T(8,128)}), s32[1024,8,16]{0,2,1:T(8,128)S(1)}, u32[]{:S(2)}, u32[]{:S(2)}) async-start(s32[1024,8,16]{0,2,1:T(8,128)} %bitcast), calls=%async_computation | async-start | bytes 1048576 | tf_op jit(solution)/shard_map/all_to_all | solution.py:48
  7.2 0.0 copy-done
  7.3 13.2 %all_gather.6 = f32[32768]{0:T(1024)S(1)} all-gather(f32[4096]{0:T(1024)S(1)} %copy-done), channel_id=1, replica_groups=mesh['rows'=8,'feat'=4] {'rows'}, dimensions={0}, use_global_device_ids=true | all-gather | bytes 147456 | tf_op jit(solution)/shard_map/all_gather | solution.py:49
  20.5 0.0 all-to-all-done
  20.5 0.3 and_bitcast_fusion.4
  20.7 0.3 copy.35
  21.1 0.1 and.76
  21.2 0.3 copy.36
  21.5 0.1 and.79
  21.6 0.3 copy.37
  21.9 0.9 %and.82 = s32[8192,1,16]{0,2,1:T(8,128)} reshape(s32[8,1024,16]{1,0,2:T(8,128)S(1)} %copy.37) | data formatting | bytes 1048576 | tf_op jit(solution)/shard_map/and | solution.py:11
  22.8 0.3 copy.38
  23.1 0.9 %and.85 = s32[8192,1,16]{0,2,1:T(8,128)} reshape(s32[8,1024,16]{1,0,2:T(8,128)S(1)} %copy.38) | data formatting | bytes 1048576 | tf_op jit(solution)/shard_map/and | solution.py:11
  24.0 1.3 %pad_add_fusion = s32[8192,4,16]{0,2,1:T(8,128)S(1)} fusion(s32[8192,1,16]{0,2,1:T(8,128)} %and.85, s32[8192,1,16]{0,2,1:T(8,128)} %and.82, s32[8192,1,16]{0,2,1:T(8,128)S(1)} %and.79, s32[8192,1,16]{0,2,1:T(8,128)S(1)} %and.76), kind=kLoop, calls=%fused_computation.14 | loop fusion | flops 1572864 | bytes 4194304 | tf_op jit(solution)/shard_map/stack | solution.py:12
  25.4 10.7 %copy.39 = s32[8192,4,16]{2,1,0:T(4,128)} copy(s32[8192,4,16]{0,2,1:T(8,128)S(1)} %pad_add_fusion) | data formatting | bytes 4194304 | tf_op jit(solution)/shard_map/stack | solution.py:12
  36.1 9.6 %copy.40 = s32[8,4096,16]{1,2,0:T(8,128)S(1)} copy(s32[8,4096,16]{2,1,0:T(8,128)} %bitcast.35) | data formatting | bytes 4194304
  45.7 0.0 copy-start.1
  45.7 27.9 %while.12 = (s32[]{:T(128)}, f32[16,16,16]{2,1,0:T(8,128)S(1)}, s32[8,4096,16]{1,2,0:T(8,128)S(1)}, f32[8,4096]{1,0:T(8,128)S(1)}, s32[]{:T(128)}, /*index=5*/s32[]{:T(128)}) while((s32[]{:T(128)}, f32[16,16,16]{2,1,0:T(8,128)S(1)}, s32[8,4096,16]{1,2,0:T(8,128)S(1)}, f32[8,4096]{1,0:T(8,128)S(1)}, s32[]{:T(128)}, ...), condition=%wide.region_1.2_spmd.clone.clone, body=%wide.region_0.1_spmd.clone.clone.sunk | while | flops 204611584 | bytes 1392727 | solution.py:34
  45.8 3.4 %fusion.16 = f32[16,16,16]{2,1,0:T(8,128)S(1)} fusion(s32[4096,16]{0,1:T(8,128)S(1)} %get-tuple-element.126, f32[4096]{0:T(1024)S(1)} %bitcast.36, s32[4096,16]{0,1:T(8,128)S(1)} %get-tuple-element.127, f32[16,16,16]{2,1,0:T(8,128)S(1)} %get-tuple-element.135, pred[]{:T(512)S(6)} %compare.3), kind=kOutput, calls=%fused_computation.9.clone.1 | convolution fusion | flops 204480512 | bytes 573441 | tf_op jit(solution)/shard_map/while/body/eval_jaxpr/rkh,rkl->khl/dot_general | solution.py:30
  49.3 3.4 %fusion.16 = f32[16,16,16]{2,1,0:T(8,128)S(1)} fusion(s32[4096,16]{0,1:T(8,128)S(1)} %get-tuple-element.126, f32[4096]{0:T(1024)S(1)} %bitcast.36, s32[4096,16]{0,1:T(8,128)S(1)} %get-tuple-element.127, f32[16,16,16]{2,1,0:T(8,128)S(1)} %get-tuple-element.135, pred[]{:T(512)S(6)} %compare.3), kind=kOutput, calls=%fused_computation.9.clone.1 | convolution fusion | flops 204480512 | bytes 573441 | tf_op jit(solution)/shard_map/while/body/eval_jaxpr/rkh,rkl->khl/dot_general | solution.py:30
  52.8 3.4 %fusion.16 = f32[16,16,16]{2,1,0:T(8,128)S(1)} fusion(s32[4096,16]{0,1:T(8,128)S(1)} %get-tuple-element.126, f32[4096]{0:T(1024)S(1)} %bitcast.36, s32[4096,16]{0,1:T(8,128)S(1)} %get-tuple-element.127, f32[16,16,16]{2,1,0:T(8,128)S(1)} %get-tuple-element.135, pred[]{:T(512)S(6)} %compare.3), kind=kOutput, calls=%fused_computation.9.clone.1 | convolution fusion | flops 204480512 | bytes 573441 | tf_op jit(solution)/shard_map/while/body/eval_jaxpr/rkh,rkl->khl/dot_general | solution.py:30
  56.2 3.4 %fusion.16 = f32[16,16,16]{2,1,0:T(8,128)S(1)} fusion(s32[4096,16]{0,1:T(8,128)S(1)} %get-tuple-element.126, f32[4096]{0:T(1024)S(1)} %bitcast.36, s32[4096,16]{0,1:T(8,128)S(1)} %get-tuple-element.127, f32[16,16,16]{2,1,0:T(8,128)S(1)} %get-tuple-element.135, pred[]{:T(512)S(6)} %compare.3), kind=kOutput, calls=%fused_computation.9.clone.1 | convolution fusion | flops 204480512 | bytes 573441 | tf_op jit(solution)/shard_map/while/body/eval_jaxpr/rkh,rkl->khl/dot_general | solution.py:30
  59.7 3.4 %fusion.16 = f32[16,16,16]{2,1,0:T(8,128)S(1)} fusion(s32[4096,16]{0,1:T(8,128)S(1)} %get-tuple-element.126, f32[4096]{0:T(1024)S(1)} %bitcast.36, s32[4096,16]{0,1:T(8,128)S(1)} %get-tuple-element.127, f32[16,16,16]{2,1,0:T(8,128)S(1)} %get-tuple-element.135, pred[]{:T(512)S(6)} %compare.3), kind=kOutput, calls=%fused_computation.9.clone.1 | convolution fusion | flops 204480512 | bytes 573441 | tf_op jit(solution)/shard_map/while/body/eval_jaxpr/rkh,rkl->khl/dot_general | solution.py:30
  63.2 3.4 %fusion.16 = f32[16,16,16]{2,1,0:T(8,128)S(1)} fusion(s32[4096,16]{0,1:T(8,128)S(1)} %get-tuple-element.126, f32[4096]{0:T(1024)S(1)} %bitcast.36, s32[4096,16]{0,1:T(8,128)S(1)} %get-tuple-element.127, f32[16,16,16]{2,1,0:T(8,128)S(1)} %get-tuple-element.135, pred[]{:T(512)S(6)} %compare.3), kind=kOutput, calls=%fused_computation.9.clone.1 | convolution fusion | flops 204480512 | bytes 573441 | tf_op jit(solution)/shard_map/while/body/eval_jaxpr/rkh,rkl->khl/dot_general | solution.py:30
  66.7 3.4 %fusion.16 = f32[16,16,16]{2,1,0:T(8,128)S(1)} fusion(s32[4096,16]{0,1:T(8,128)S(1)} %get-tuple-element.126, f32[4096]{0:T(1024)S(1)} %bitcast.36, s32[4096,16]{0,1:T(8,128)S(1)} %get-tuple-element.127, f32[16,16,16]{2,1,0:T(8,128)S(1)} %get-tuple-element.135, pred[]{:T(512)S(6)} %compare.3), kind=kOutput, calls=%fused_computation.9.clone.1 | convolution fusion | flops 204480512 | bytes 573441 | tf_op jit(solution)/shard_map/while/body/eval_jaxpr/rkh,rkl->khl/dot_general | solution.py:30
  70.2 3.4 %fusion.16 = f32[16,16,16]{2,1,0:T(8,128)S(1)} fusion(s32[4096,16]{0,1:T(8,128)S(1)} %get-tuple-element.126, f32[4096]{0:T(1024)S(1)} %bitcast.36, s32[4096,16]{0,1:T(8,128)S(1)} %get-tuple-element.127, f32[16,16,16]{2,1,0:T(8,128)S(1)} %get-tuple-element.135, pred[]{:T(512)S(6)} %compare.3), kind=kOutput, calls=%fused_computation.9.clone.1 | convolution fusion | flops 204480512 | bytes 573441 | tf_op jit(solution)/shard_map/while/body/eval_jaxpr/rkh,rkl->khl/dot_general | solution.py:30
  73.6 0.1 reshape.161
  73.7 0.1 reshape.163
  73.8 0.6 reduce-window.6
  74.4 0.2 slice_reduce_fusion
  74.6 0.1 copy_bitcast_fusion
  74.7 0.1 fusion.12
  74.8 0.2 slice_reduce_fusion.1
  75.0 0.0 copy-done.1
  75.0 0.1 broadcast_multiply_fusion
  75.0 0.7 clamp_reduce_fusion
  75.7 8.3 %all_gather.7 = f32[128,128]{1,0:T(8,128)S(1)} all-gather(f32[16,128]{1,0:T(8,128)S(1)} %clamp_reduce_fusion), channel_id=1, replica_groups=mesh['rows'=8,'feat'=4] {'rows'}, dimensions={0}, use_global_device_ids=true | all-gather | bytes 73728 | tf_op jit(solution)/shard_map/all_gather | solution.py:52
  84.0 0.6 copy.54
  (21 shorter events, 0.6 us)
Async XLA Ops:
  0.0 7.2 %copy-start = (f32[4096]{0:T(1024)S(1)}, f32[4096]{0:T(1024)}, u32[]{:S(2)}) copy-start(f32[4096]{0:T(1024)} %param.6) | copy-start | bytes 49156
  2.0 18.4 %all-to-all-start = ((s32[1024,8,16]{0,2,1:T(8,128)}), s32[1024,8,16]{0,2,1:T(8,128)S(1)}, u32[]{:S(2)}, u32[]{:S(2)}) async-start(s32[1024,8,16]{0,2,1:T(8,128)} %bitcast), calls=%async_computation | async-start | bytes 1048576 | tf_op jit(solution)/shard_map/all_to_all | solution.py:48
  45.7 29.3 %copy-start.1 = (f32[128]{0:T(128)S(1)}, f32[128]{0:T(128)}, u32[]{:S(2)}) copy-start(f32[128]{0:T(128)} %param.7) | copy-start | bytes 1540
where the time goes:
time: 85 us; the launch traced here: 84.6 us
  matrix products  27.1 us (32%)
  local copies, waits for them, and re-layouts  27 us (32%)
  blocking collectives  21.5 us (25%)
  starting transfers between devices  5.2 us (6%)
  other arithmetic  3.46 us (4%)
    dot_general x8, matrix products, add_block(): jnp.einsum('rkh,rkl->khl', high_hot, low_hot, precision=lax.Precision.HIG...  27.1 us
    all_gather x1, blocking collectives, local(): weights = lax.all_gather(hessian, 'rows', axis=0, tiled=True)  13.2 us
    unnamed x7, local copies, waits for them, and re-layouts  12.3 us
    another operation x1, local copies, waits for them, and re-layouts, unpack(): stacked = jnp.stack(parts, axis=1)  10.7 us
    all_gather x1, blocking collectives, local(): return lax.all_gather(cuts, 'rows', axis=0, tiled=True)  8.29 us
    all_to_all x1, starting transfers between devices, local(): lax.all_to_all(bins, 'rows', split_axis=1, concat_axis=0, tiled=True)  5.2 us
    and x8, local copies, waits for them, and re-layouts, unpack(): jnp.bitwise_and(jnp.right_shift(words, 8 * k), 255)  3.23 us
  transfers between devices with their start and end apart: 1, of which 0 were waited for; matrix products, arithmetic and copies ran while one was open for 0% of the time, Pallas kernels for 0%

commit v1 on v0

--- a/solution.py
+++ b/solution.py
@@ -5,6 +5,15 @@
 from jax.sharding import PartitionSpec as P
 
 BINS = 256
+register_the_roads = lambda m, dim_no: jnp.concatenate(
+    lax.all_to_all(
+        jnp.stack([m for _ in range(lax.axis_size("rows"))], 0),
+        axis_name="rows",
+        split_axis=0,
+        concat_axis=0,
+    ),
+    dim_no,
+)
 
 
 def unpack(words):
@@ -49,7 +58,7 @@
     weights = lax.all_gather(hessian, "rows", axis=0, tiled=True)
     hist = histogram(unpack(regrouped), weights)
     cuts = cut_positions(hist, thresholds)
-    return lax.all_gather(cuts, "rows", axis=0, tiled=True)
+    return register_the_roads(cuts, 0)
 
 
 def solution(mesh):

time: 85 us -> 84.3 us (level)
    all_gather x1 -> x0, blocking collectives: 8.29 us -> none  [local(): return lax.all_gather(cuts, 'rows', axis=0, tiled=True)]
    all_to_all x0 -> x1, blocking collectives: none -> 7.54 us  [lax.all_to_all(jnp.stack([m for _ in range(lax.axis_size('rows'))], 0), a...]
where the time goes in v1:
time: 84.3 us; the launch traced here: 83.9 us
  matrix products  27.1 us (32%)
  local copies, waits for them, and re-layouts  27 us (32%)
  blocking collectives  20.7 us (25%)
  starting transfers between devices  5.2 us (6%)
  other arithmetic  3.46 us (4%)
    dot_general x8, matrix products, add_block(): jnp.einsum('rkh,rkl->khl', high_hot, low_hot, precision=lax.Precision.HIG...  27.1 us
    all_gather x1, blocking collectives, local(): weights = lax.all_gather(hessian, 'rows', axis=0, tiled=True)  13.2 us
    unnamed x7, local copies, waits for them, and re-layouts  12.3 us
    another operation x1, local copies, waits for them, and re-layouts, unpack(): stacked = jnp.stack(parts, axis=1)  10.7 us
    all_to_all x1, blocking collectives, lax.all_to_all(jnp.stack([m for _ in range(lax.axis_size('rows'))], 0), a...  7.54 us
    all_to_all x1, starting transfers between devices, local(): lax.all_to_all(bins, 'rows', split_axis=1, concat_axis=0, tiled=True)  5.2 us
    and x8, local copies, waits for them, and re-layouts, unpack(): jnp.bitwise_and(jnp.right_shift(words, 8 * k), 255)  3.23 us
  transfers between devices with their start and end apart: 1, of which 0 were waited for; matrix products, arithmetic and copies ran while one was open for 0% of the time, Pallas kernels for 0%

profile of v1, /device:TPU:0, one launch (start us, length us, event | category | flops | bytes accessed | tf_op | source)
XLA Modules:
  0.0 83.9 jit_solution(6978148942795891849)
XLA Ops:
  0.0 0.0 copy-start
  0.0 2.0 %copy.34 = s32[1024,128]{0,1:T(8,128)} copy(s32[1024,128]{1,0:T(8,128)} %param.5) | data formatting | bytes 1048576 | tf_op args[0]
  2.0 5.2 %all-to-all-start = ((s32[1024,8,16]{0,2,1:T(8,128)}), s32[1024,8,16]{0,2,1:T(8,128)S(1)}, u32[]{:S(2)}, u32[]{:S(2)}) async-start(s32[1024,8,16]{0,2,1:T(8,128)} %bitcast), calls=%async_computation | async-start | bytes 1048576 | tf_op jit(solution)/shard_map/all_to_all | solution.py:57
  7.2 0.0 copy-done
  7.3 13.2 %all_gather.3 = f32[32768]{0:T(1024)S(1)} all-gather(f32[4096]{0:T(1024)S(1)} %copy-done), channel_id=1, replica_groups=mesh['rows'=8,'feat'=4] {'rows'}, dimensions={0}, use_global_device_ids=true | all-gather | bytes 147456 | tf_op jit(solution)/shard_map/all_gather | solution.py:58
  20.5 0.0 all-to-all-done
  20.5 0.3 and_bitcast_fusion.4
  20.7 0.3 copy.35
  21.1 0.1 and.76
  21.2 0.3 copy.36
  21.5 0.1 and.79
  21.6 0.3 copy.37
  21.9 0.9 %and.82 = s32[8192,1,16]{0,2,1:T(8,128)} reshape(s32[8,1024,16]{1,0,2:T(8,128)S(1)} %copy.37) | data formatting | bytes 1048576 | tf_op jit(solution)/shard_map/and | solution.py:20
  22.8 0.3 copy.38
  23.1 0.9 %and.85 = s32[8192,1,16]{0,2,1:T(8,128)} reshape(s32[8,1024,16]{1,0,2:T(8,128)S(1)} %copy.38) | data formatting | bytes 1048576 | tf_op jit(solution)/shard_map/and | solution.py:20
  24.0 1.3 %pad_add_fusion = s32[8192,4,16]{0,2,1:T(8,128)S(1)} fusion(s32[8192,1,16]{0,2,1:T(8,128)} %and.85, s32[8192,1,16]{0,2,1:T(8,128)} %and.82, s32[8192,1,16]{0,2,1:T(8,128)S(1)} %and.79, s32[8192,1,16]{0,2,1:T(8,128)S(1)} %and.76), kind=kLoop, calls=%fused_computation.14 | loop fusion | flops 1572864 | bytes 4194304 | tf_op jit(solution)/shard_map/stack | solution.py:21
  25.4 10.7 %copy.39 = s32[8192,4,16]{2,1,0:T(4,128)} copy(s32[8192,4,16]{0,2,1:T(8,128)S(1)} %pad_add_fusion) | data formatting | bytes 4194304 | tf_op jit(solution)/shard_map/stack | solution.py:21
  36.1 9.6 %copy.40 = s32[8,4096,16]{1,2,0:T(8,128)S(1)} copy(s32[8,4096,16]{2,1,0:T(8,128)} %bitcast.36) | data formatting | bytes 4194304
  45.7 0.0 copy-start.1
  45.7 27.9 %while.12 = (s32[]{:T(128)}, f32[16,16,16]{2,1,0:T(8,128)S(1)}, s32[8,4096,16]{1,2,0:T(8,128)S(1)}, f32[8,4096]{1,0:T(8,128)S(1)}, s32[]{:T(128)}, /*index=5*/s32[]{:T(128)}) while((s32[]{:T(128)}, f32[16,16,16]{2,1,0:T(8,128)S(1)}, s32[8,4096,16]{1,2,0:T(8,128)S(1)}, f32[8,4096]{1,0:T(8,128)S(1)}, s32[]{:T(128)}, ...), condition=%wide.region_1.2_spmd.clone.clone, body=%wide.region_0.1_spmd.clone.clone.sunk | while | flops 204611584 | bytes 1392727 | solution.py:43
  45.8 3.4 %fusion.16 = f32[16,16,16]{2,1,0:T(8,128)S(1)} fusion(s32[4096,16]{0,1:T(8,128)S(1)} %get-tuple-element.126, f32[4096]{0:T(1024)S(1)} %bitcast.37, s32[4096,16]{0,1:T(8,128)S(1)} %get-tuple-element.127, f32[16,16,16]{2,1,0:T(8,128)S(1)} %get-tuple-element.135, pred[]{:T(512)S(6)} %compare.3), kind=kOutput, calls=%fused_computation.9.clone.1 | convolution fusion | flops 204480512 | bytes 573441 | tf_op jit(solution)/shard_map/while/body/eval_jaxpr/rkh,rkl->khl/dot_general | solution.py:39
  49.3 3.4 %fusion.16 = f32[16,16,16]{2,1,0:T(8,128)S(1)} fusion(s32[4096,16]{0,1:T(8,128)S(1)} %get-tuple-element.126, f32[4096]{0:T(1024)S(1)} %bitcast.37, s32[4096,16]{0,1:T(8,128)S(1)} %get-tuple-element.127, f32[16,16,16]{2,1,0:T(8,128)S(1)} %get-tuple-element.135, pred[]{:T(512)S(6)} %compare.3), kind=kOutput, calls=%fused_computation.9.clone.1 | convolution fusion | flops 204480512 | bytes 573441 | tf_op jit(solution)/shard_map/while/body/eval_jaxpr/rkh,rkl->khl/dot_general | solution.py:39
  52.8 3.4 %fusion.16 = f32[16,16,16]{2,1,0:T(8,128)S(1)} fusion(s32[4096,16]{0,1:T(8,128)S(1)} %get-tuple-element.126, f32[4096]{0:T(1024)S(1)} %bitcast.37, s32[4096,16]{0,1:T(8,128)S(1)} %get-tuple-element.127, f32[16,16,16]{2,1,0:T(8,128)S(1)} %get-tuple-element.135, pred[]{:T(512)S(6)} %compare.3), kind=kOutput, calls=%fused_computation.9.clone.1 | convolution fusion | flops 204480512 | bytes 573441 | tf_op jit(solution)/shard_map/while/body/eval_jaxpr/rkh,rkl->khl/dot_general | solution.py:39
  56.2 3.4 %fusion.16 = f32[16,16,16]{2,1,0:T(8,128)S(1)} fusion(s32[4096,16]{0,1:T(8,128)S(1)} %get-tuple-element.126, f32[4096]{0:T(1024)S(1)} %bitcast.37, s32[4096,16]{0,1:T(8,128)S(1)} %get-tuple-element.127, f32[16,16,16]{2,1,0:T(8,128)S(1)} %get-tuple-element.135, pred[]{:T(512)S(6)} %compare.3), kind=kOutput, calls=%fused_computation.9.clone.1 | convolution fusion | flops 204480512 | bytes 573441 | tf_op jit(solution)/shard_map/while/body/eval_jaxpr/rkh,rkl->khl/dot_general | solution.py:39
  59.7 3.4 %fusion.16 = f32[16,16,16]{2,1,0:T(8,128)S(1)} fusion(s32[4096,16]{0,1:T(8,128)S(1)} %get-tuple-element.126, f32[4096]{0:T(1024)S(1)} %bitcast.37, s32[4096,16]{0,1:T(8,128)S(1)} %get-tuple-element.127, f32[16,16,16]{2,1,0:T(8,128)S(1)} %get-tuple-element.135, pred[]{:T(512)S(6)} %compare.3), kind=kOutput, calls=%fused_computation.9.clone.1 | convolution fusion | flops 204480512 | bytes 573441 | tf_op jit(solution)/shard_map/while/body/eval_jaxpr/rkh,rkl->khl/dot_general | solution.py:39
  63.2 3.4 %fusion.16 = f32[16,16,16]{2,1,0:T(8,128)S(1)} fusion(s32[4096,16]{0,1:T(8,128)S(1)} %get-tuple-element.126, f32[4096]{0:T(1024)S(1)} %bitcast.37, s32[4096,16]{0,1:T(8,128)S(1)} %get-tuple-element.127, f32[16,16,16]{2,1,0:T(8,128)S(1)} %get-tuple-element.135, pred[]{:T(512)S(6)} %compare.3), kind=kOutput, calls=%fused_computation.9.clone.1 | convolution fusion | flops 204480512 | bytes 573441 | tf_op jit(solution)/shard_map/while/body/eval_jaxpr/rkh,rkl->khl/dot_general | solution.py:39
  66.7 3.4 %fusion.16 = f32[16,16,16]{2,1,0:T(8,128)S(1)} fusion(s32[4096,16]{0,1:T(8,128)S(1)} %get-tuple-element.126, f32[4096]{0:T(1024)S(1)} %bitcast.37, s32[4096,16]{0,1:T(8,128)S(1)} %get-tuple-element.127, f32[16,16,16]{2,1,0:T(8,128)S(1)} %get-tuple-element.135, pred[]{:T(512)S(6)} %compare.3), kind=kOutput, calls=%fused_computation.9.clone.1 | convolution fusion | flops 204480512 | bytes 573441 | tf_op jit(solution)/shard_map/while/body/eval_jaxpr/rkh,rkl->khl/dot_general | solution.py:39
  70.2 3.4 %fusion.16 = f32[16,16,16]{2,1,0:T(8,128)S(1)} fusion(s32[4096,16]{0,1:T(8,128)S(1)} %get-tuple-element.126, f32[4096]{0:T(1024)S(1)} %bitcast.37, s32[4096,16]{0,1:T(8,128)S(1)} %get-tuple-element.127, f32[16,16,16]{2,1,0:T(8,128)S(1)} %get-tuple-element.135, pred[]{:T(512)S(6)} %compare.3), kind=kOutput, calls=%fused_computation.9.clone.1 | convolution fusion | flops 204480512 | bytes 573441 | tf_op jit(solution)/shard_map/while/body/eval_jaxpr/rkh,rkl->khl/dot_general | solution.py:39
  73.6 0.1 reshape.166
  73.7 0.1 reshape.168
  73.8 0.6 reduce-window.6
  74.4 0.2 slice_reduce_fusion
  74.6 0.1 copy_bitcast_fusion
  74.7 0.1 fusion.12
  74.8 0.2 slice_reduce_fusion.1
  75.0 0.0 copy-done.1
  75.0 0.1 broadcast_multiply_fusion
  75.0 0.7 clamp_reduce_fusion
  75.7 7.5 %all_to_all.18 = f32[8,16,128]{2,1,0:T(8,128)S(1)} all-to-all(f32[8,16,128]{2,1,0:T(8,128)S(1)} %stack.5), channel_id=1, replica_groups=mesh['rows'=8,'feat'=4] {'rows'}, dimensions={0} | all-to-all | bytes 131072 | tf_op jit(solution)/shard_map/all_to_all | solution.py:9
  83.3 0.6 copy.54
  (22 shorter events, 0.6 us)
Async XLA Ops:
  0.0 7.2 %copy-start = (f32[4096]{0:T(1024)S(1)}, f32[4096]{0:T(1024)}, u32[]{:S(2)}) copy-start(f32[4096]{0:T(1024)} %param.6) | copy-start | bytes 49156
  2.0 18.4 %all-to-all-start = ((s32[1024,8,16]{0,2,1:T(8,128)}), s32[1024,8,16]{0,2,1:T(8,128)S(1)}, u32[]{:S(2)}, u32[]{:S(2)}) async-start(s32[1024,8,16]{0,2,1:T(8,128)} %bitcast), calls=%async_computation | async-start | bytes 1048576 | tf_op jit(solution)/shard_map/all_to_all | solution.py:57
  45.7 29.3 %copy-start.1 = (f32[128]{0:T(128)S(1)}, f32[128]{0:T(128)}, u32[]{:S(2)}) copy-start(f32[128]{0:T(128)} %param.7) | copy-start | bytes 1540
